TPU v7x, 32 devices: a whole 2x2x4 slice. The times are simulated.
32 devices in a mesh: row: 2 (over x), col: 16 (over z, y, core).
Axes of the slice: x: 2, y: 2, z: 4, core: 2. Of those that a mesh axis runs over, the one named last changes fastest.
Arguments:
- tokens: bfloat16 [64, 128, 1024], P('row', 'col'), may hold values from -6 to 6
- shifts: int32 [2], replicated, may hold values from 0 to 15
- qkv_weight: bfloat16 [1024, 3, 1024], P('col', None, 'row'), may hold values from -0.1875 to 0.1875
- out_weight: bfloat16 [1024, 1024], P('row', 'col'), may hold values from -0.1875 to 0.1875
- up_weight: bfloat16 [1024, 4096], P('col', 'row'), may hold values from -0.1875 to 0.1875
- down_weight: bfloat16 [4096, 1024], P('row', 'col'), may hold values from -0.09375 to 0.09375
- qk_gain: float32 [1024], P('row'), may hold values from 0.5 to 1.5
- attn_rate: float32 [1024], replicated, may hold values from 0.1 to 0.6
- mlp_rate: float32 [1024], replicated, may hold values from 0.1 to 0.6
- hidden_gain: float32 [4096], P('row'), may hold values from 0.5 to 2
Outputs:
- sphere_out: bfloat16 [64, 128, 1024], P('row', 'col')
Inputs may be any that keep to these rules, and one draw needn't show every extreme that they name: shifts[0] offsets the windows along rows, shifts[1] along columns.
All inputs are finite; a program needn't handle non-finite values.
Results may differ from a plain program's by a relative error of at most 0.012.
Values may be sent and summed in bfloat16 or wider, within the bound.
A program may use at most 128 MiB of HBM per device.

v0:
```python
import functools
import math

import jax
import jax.numpy as jnp
from jax import lax
from jax.experimental import pallas as pl
from jax.experimental.pallas import tpu as pltpu
from jax.sharding import PartitionSpec as P

HD = 64
WIN = 16
MESH = pl.DeviceIdType.MESH
VMEM = pl.BlockSpec(memory_space=pltpu.VMEM)


def shifted(value, axis, steps):
    count = lax.axis_size(axis)
    pairs = [(source, (source + steps) % count) for source in range(count)]
    return lax.ppermute(value, axis, pairs)


def to_sphere(vector):
    return vector * lax.rsqrt(jnp.mean(vector * vector, axis=-1, keepdims=True) + 1e-06)


def gather_kernel(n_row, n_col, reach, n_weights, *refs):
    tok_in = refs[0]
    w_in = refs[1 : 1 + n_weights]
    tok_out = refs[1 + n_weights]
    w_out = refs[2 + n_weights : 2 + 2 * n_weights]
    send_sem, recv_sem = refs[2 + 2 * n_weights :]
    row = lax.axis_index("row")
    col = lax.axis_index("col")
    nz = n_col // 4
    z = col // 4
    y = (col // 2) % 2
    core = col % 2

    def at(zz, yy, cc):
        return (lax.rem(zz + 2 * nz, nz) * 2 + yy) * 2 + cc

    z_next = at(z + 1, y, core)
    z_prev = at(z - 1, y, core)
    y_peer = at(z, 1 - y, core)
    core_peer = at(z, y, 1 - core)
    greet = [(row, z_next), (row, z_prev), (row, y_peer), (row, core_peer)]
    for k in range(1, reach + 1):
        greet.append((row, lax.rem(col + k, n_col)))
        greet.append((row, lax.rem(col - k + n_col, n_col)))
    for r in range(1, n_row):
        greet.append((lax.rem(row + r, n_row), col))
    barrier = pltpu.get_barrier_semaphore()
    for peer in greet:
        pl.semaphore_signal(barrier, inc=1, device_id=peer, device_id_type=MESH)
    pl.semaphore_wait(barrier, len(greet))

    started = []

    def send(src, dst, peer):
        index = len(started)
        copy = pltpu.make_async_remote_copy(
            src_ref=src,
            dst_ref=dst,
            send_sem=send_sem.at[index],
            recv_sem=recv_sem.at[index],
            device_id=peer,
            device_id_type=MESH,
        )
        copy.start()
        started.append(copy)
        return copy

    near = {}
    far = []
    for r in range(1, n_row):
        far.append(send(tok_in, tok_out.at[row, 0], (lax.rem(row + r, n_row), col)))
    for k in range(1, reach + 1):
        near[k] = send(tok_in, tok_out.at[row, k], (row, lax.rem(col - k + n_col, n_col)))
    z_copy, y_copy, core_copies = {}, {}, []
    for w in range(n_weights):
        z_copy[w, 0] = send(w_in[w], w_out[w].at[col], (row, z_next))
        y_copy[w, 0] = send(w_in[w], w_out[w].at[col], (row, y_peer))
        core_copies.append(send(w_in[w], w_out[w].at[col], (row, core_peer)))
    tok_out[row, 0] = tok_in[...]
    for w in range(n_weights):
        w_out[w][col] = w_in[w][...]
    for t in range(nz):
        for w in range(n_weights):
            if t > 0:
                z_copy[w, t - 1].wait_recv()
                block = w_out[w].at[at(z - t, y, core)]
                if t < nz - 1:
                    z_copy[w, t] = send(block, block, (row, z_next))
                y_copy[w, t] = send(block, block, (row, y_peer))
                core_copies.append(send(block, block, (row, core_peer)))
            y_copy[w, t].wait_recv()
            other = w_out[w].at[at(z - t, 1 - y, core)]
            core_copies.append(send(other, other, (row, core_peer)))
        if t == 0:
            for k in range(1, reach + 1):
                near[k].wait_recv()
                piece = tok_out.at[row, k]
                for r in range(1, n_row):
                    far.append(send(piece, piece, (lax.rem(row + r, n_row), col)))
    for copy in far:
        copy.wait_recv()
    for copy in core_copies:
        copy.wait_recv()
    for copy in started:
        copy.wait_send()


def gather_all(tokens, weights, n_row, n_col, reach):
    nz = n_col // 4
    n_weights = len(weights)
    copies = reach * n_row + (n_row - 1) + n_weights * (nz - 1 + nz + 2 * nz)
    return pl.pallas_call(
        functools.partial(gather_kernel, n_row, n_col, reach, n_weights),
        out_shape=[jax.ShapeDtypeStruct((n_row, reach + 1) + tokens.shape, tokens.dtype)]
        + [jax.ShapeDtypeStruct((n_col,) + w.shape, w.dtype) for w in weights],
        in_specs=[VMEM] * (1 + n_weights),
        out_specs=[VMEM] * (1 + n_weights),
        scratch_shapes=[pltpu.SemaphoreType.DMA((copies,)), pltpu.SemaphoreType.DMA((copies,))],
        compiler_params=pltpu.CompilerParams(
            collective_id=0, has_side_effects=True, vmem_limit_bytes=48 * 1024 * 1024
        ),
        name="gather_all",
    )(tokens, *weights)


def project_kernel(heads, x_ref, w_ref, gain_ref, q_ref, kv_ref):
    width = heads * HD
    projected = jnp.dot(x_ref[...], w_ref[...], preferred_element_type=jnp.float32)
    for part in range(2):
        for head in range(heads):
            lo = head * HD
            piece = projected[:, part * width + lo : part * width + lo + HD]
            scaled = (to_sphere(piece) * gain_ref[:, lo : lo + HD]).astype(jnp.bfloat16)
            if part == 0:
                q_ref[:, lo : lo + HD] = scaled
            else:
                kv_ref[0, :, lo : lo + HD] = scaled
    kv_ref[1] = projected[:, 2 * width :].astype(jnp.bfloat16)


def project(x, weight, gain, heads):
    tokens, depth = x.shape
    width = heads * HD
    block = math.gcd(tokens, 128)
    return pl.pallas_call(
        functools.partial(project_kernel, heads),
        grid=(tokens // block,),
        out_shape=[
            jax.ShapeDtypeStruct((tokens, width), jnp.bfloat16),
            jax.ShapeDtypeStruct((2, tokens, width), jnp.bfloat16),
        ],
        in_specs=[
            pl.BlockSpec((block, depth), lambda i: (i, 0)),
            pl.BlockSpec((depth, 3 * width), lambda i: (0, 0)),
            pl.BlockSpec((1, width), lambda i: (0, 0)),
        ],
        out_specs=[
            pl.BlockSpec((block, width), lambda i: (i, 0)),
            pl.BlockSpec((2, block, width), lambda i: (0, i, 0)),
        ],
        name="project",
        cost_estimate=pl.CostEstimate(
            flops=6 * tokens * depth * width, bytes_accessed=8 * depth * width, transcendentals=0
        ),
    )(x, weight, gain.reshape(1, width))


def attend_kernel(heads, q_ref, *refs):
    out_ref = refs[-1]
    kv_refs = refs[:-1]
    contract = (((1,), (1,)), ((), ()))
    for head in range(heads):
        cut = slice(head * HD, head * HD + HD)
        query = q_ref[:, cut]
        keys = jnp.concatenate([kv[0, :, cut] for kv in kv_refs], axis=0)
        values = jnp.concatenate([kv[1, :, cut] for kv in kv_refs], axis=0)
        scores = lax.dot_general(query, keys, contract, preferred_element_type=jnp.float32)
        expo = jnp.exp(scores * (1.0 / math.sqrt(HD)))
        weights = (expo / jnp.sum(expo, axis=-1, keepdims=True)).astype(jnp.bfloat16)
        out_ref[:, cut] = jnp.dot(weights, values, preferred_element_type=jnp.float32).astype(
            jnp.bfloat16
        )


def attend(queries, kv_parts, heads, band):
    tokens, width = queries.shape
    return pl.pallas_call(
        functools.partial(attend_kernel, heads),
        grid=(tokens // band,),
        out_shape=jax.ShapeDtypeStruct((tokens, width), jnp.bfloat16),
        in_specs=[pl.BlockSpec((band, width), lambda i: (i, 0))]
        + [pl.BlockSpec((2, band, width), lambda i: (0, i, 0)) for _ in kv_parts],
        out_specs=pl.BlockSpec((band, width), lambda i: (i, 0)),
        name="attend",
        cost_estimate=pl.CostEstimate(
            flops=4 * tokens * band * width * len(kv_parts),
            bytes_accessed=6 * tokens * width,
            transcendentals=tokens * band * heads * len(kv_parts),
        ),
    )(queries, *kv_parts)


def on_device(
    tokens,
    shifts,
    qkv_weight,
    out_weight,
    up_weight,
    down_weight,
    qk_gain,
    attn_rate,
    mlp_rate,
    hidden_gain,
):
    n_row = lax.axis_size("row")
    n_col = lax.axis_size("col")
    row = lax.axis_index("row")
    local_rows, cols, width = tokens.shape
    local_width = qkv_weight.shape[2]
    hidden = up_weight.shape[1]
    heads = local_width // HD
    per_window = WIN // cols
    reach = (WIN + cols - 2) // cols
    strip_rows = local_rows * n_row
    count = strip_rows * cols
    shift_row, shift_col = shifts[0], shifts[1]

    gathered = gather_all(
        tokens.reshape(local_rows * cols, width),
        [
            qkv_weight.reshape(-1, 3 * local_width),
            out_weight.T,
            up_weight,
            down_weight.T,
        ],
        n_row,
        n_col,
        reach,
    )
    pieces = gathered[0].reshape(n_row, reach + 1, local_rows, cols, width)
    qkv_full = gathered[1].reshape(width, 3 * local_width)
    out_full = gathered[2].reshape(width, local_width)
    up_full = gathered[3].reshape(width, hidden)
    down_full = gathered[4].reshape(width, hidden)

    wide = pieces.transpose(0, 2, 1, 3, 4).reshape(strip_rows, (reach + 1) * cols, width)
    strip = lax.dynamic_slice_in_dim(wide, shift_col, cols, axis=1)
    normed = to_sphere(strip.astype(jnp.float32))
    flat = normed.reshape(count, width)
    rolled = jnp.roll(normed.astype(jnp.bfloat16), -shift_row, axis=0).reshape(count, width)
    queries, kv = project(rolled, qkv_full, qk_gain, heads)
    kv_parts = [kv]
    for k in range(1, per_window):
        pairs = [
            (c, c // per_window * per_window + (c + k) % per_window) for c in range(n_col)
        ]
        kv_parts.append(lax.ppermute(kv, "col", pairs))
    attended = attend(queries, kv_parts, heads, WIN * cols)
    attended = jnp.roll(
        attended.reshape(strip_rows, cols, local_width), shift_row, axis=0
    ).reshape(count, local_width)
    contract = (((1,), (1,)), ((), ()))
    attn_own = lax.dot_general(
        attended, out_full, contract, preferred_element_type=jnp.float32
    ).astype(jnp.bfloat16)
    attn_all = attn_own.astype(jnp.float32)
    for r in range(1, n_row):
        attn_all = attn_all + shifted(attn_own, "row", r).astype(jnp.float32)
    mixed = to_sphere(flat + attn_rate * (to_sphere(attn_all) - flat))
    raised = jnp.dot(mixed.astype(jnp.bfloat16), up_full, preferred_element_type=jnp.float32)
    activated = jax.nn.gelu(raised * hidden_gain, approximate=False).astype(jnp.bfloat16)
    mlp_own = lax.dot_general(
        activated, down_full, contract, preferred_element_type=jnp.float32
    ).astype(jnp.bfloat16)
    local = local_rows * cols

    def part(value, owner):
        return lax.dynamic_slice_in_dim(value, owner * local, local, 0)

    mlp_local = part(mlp_own, row).astype(jnp.float32)
    for r in range(1, n_row):
        there = part(mlp_own, lax.rem(row + r, n_row))
        mlp_local = mlp_local + shifted(there, "row", r).astype(jnp.float32)
    mixed_local = part(mixed, row)
    result = to_sphere(mixed_local + mlp_rate * (to_sphere(mlp_local) - mixed_local))
    result = result.astype(jnp.bfloat16).reshape(local_rows, cols, width)
    spread = [shifted(result, "col", k) for k in range(reach, 0, -1)] + [result]
    spread = jnp.concatenate(spread, axis=1)
    return lax.dynamic_slice_in_dim(spread, reach * cols - shift_col, cols, axis=1)


def solution(mesh):
    return jax.shard_map(
        on_device,
        mesh=mesh,
        in_specs=(
            P("row", "col", None),
            P(),
            P("col", None, "row"),
            P("row", "col"),
            P("col", "row"),
            P("row", "col"),
            P("row"),
            P(),
            P(),
            P("row"),
        ),
        out_specs=P("row", "col", None),
        check_vma=False,
    )
```

profile of v0, /device:TPU:0, one launch (start us, length us, event | category | flops | bytes accessed | tf_op | source)
XLA Modules:
  0.0 245.8 jit_solution(9669441095166041695)
XLA Ops:
  0.0 1.3 fusion.60
  2.6 0.9 copy.22
  3.5 0.0 copy-start
  3.5 1.0 copy-done
  4.6 0.0 copy-start.1
  4.6 0.9 copy-done.1
  5.5 0.0 copy-start.2
  5.5 0.9 copy-done.2
  6.5 0.0 copy-start.3
  6.5 0.8 copy-done.3
  7.3 114.9 %gather_all.1 = (bf16[2,3,256,1024]{3,2,1,0:T(8,128)(2,1)S(1)}, bf16[16,64,1536]{2,1,0:T(8,128)(2,1)}, bf16[16,64,512]{2,1,0:T(8,128)(2,1)S(1)}, bf16[16,64,2048]{2,1,0:T(8,128)(2,1)}, bf16[16,64,2048]{2,1,0:T(8,128)(2,1)}) custom-call(bf16[256,1024]{1,0:T(8,128)(2,1)S(1)} %bitcast.43, bf16[64,1536]{1,0:T(8,128)(2,1)S(1)} %bitcast.42, ...), custom_call_target="tpu_custom_call" | custom-call | tf_op jit(solution)/shard_map/gather_all/pallas_call | solution.py:118
  122.2 2.1 copy.19
  126.2 2.1 fusion.15
  128.3 0.1 copy.20
  128.3 0.1 copy.21
  128.4 2.0 fusion.10
  130.4 1.5 fusion.19.x_ref
  131.9 10.1 %project.1 = (bf16[512,512]{1,0:T(8,128)(2,1)}, bf16[2,512,512]{2,1,0:T(8,128)(2,1)}) custom-call(bf16[512,1024]{1,0:T(8,128)(2,1)} %fusion.19.x_ref, bf16[1024,1536]{1,0:T(8,128)(2,1)} %bitcast.55, f32[1,512]{1,0:T(1,128)} %bitcast.56), custom_call_target="tpu_custom_call" | custom-call | flops 1610612736 | bytes 4194304 | tf_op jit(solution)/shard_map/project/pallas_call | solution.py:151
  142.0 0.5 collective-permute-start
  143.7 1.3 collective-permute-done.refs_1_
  145.0 0.0 copy-start.6
  145.0 1.0 copy-done.6
  146.0 7.0 %attend.1 = bf16[512,512]{1,0:T(8,128)(2,1)} custom-call(bf16[512,512]{1,0:T(8,128)(2,1)} %get-tuple-element.14.q_ref, bf16[2,512,512]{2,1,0:T(8,128)(2,1)} %get-tuple-element.15.refs_0_, bf16[2,512,512]{2,1,0:T(8,128)(2,1)} %copy-done.6), custom_call_target="tpu_custom_call" | custom-call | flops 268435456 | bytes 1572864 | tf_op jit(solution)/shard_map/attend/pallas_call | solution.py:193
  153.0 1.8 convolution_convert_fusion
  154.8 1.0 collective-permute-start.1
  155.8 24.5 %collective-permute-done.1 = bf16[512,1024]{1,0:T(8,128)(2,1)S(1)} collective-permute-done((bf16[512,1024]{1,0:T(8,128)(2,1)S(1)}, bf16[512,1024]{1,0:T(8,128)(2,1)S(1)}, u32[]{:S(2)}, u32[]{:S(2)}) %collective-permute-start.1) | collective-permute-done | bytes 1048608 | tf_op jit(solution)/shard_map/ppermute | solution.py:20
  180.3 0.4 multiply_reduce_fusion.1
  180.8 0.0 copy-done.8
  180.8 0.0 copy-start.9
  180.8 2.8 %multiply_reduce_fusion = f32[512]{0:T(512)S(1)} fusion(f32[512]{0:T(512)S(1)} %add_rsqrt_fusion.2, bf16[512,1024]{1,0:T(8,128)(2,1)S(1)} %collective-permute-done.1, bf16[512,1024]{1,0:T(8,128)(2,1)S(1)} %convolution_convert_fusion, f32[1024]{0:T(1024)S(1)} %copy-done.8, f32[64,8]{1,0:T(8,128)S(1)} %copy.21, bf16[64,24,1024]{2,1,0:T(8,128)(2,1)} %bitcast.49, ...), kind=kLoop, calls=%fused_computation.29 | loop fusion | flops 5766656 | bytes 3155972 | tf_op jit(solution)/shard_map/reduce_sum | solution.py:24
  183.6 3.9 %broadcast_multiply_fusion = f32[512,1024]{1,0:T(8,128)} fusion(f32[512]{0:T(512)S(1)} %add_rsqrt_fusion.1, f32[512]{0:T(512)S(1)} %add_rsqrt_fusion.2, bf16[512,1024]{1,0:T(8,128)(2,1)S(1)} %collective-permute-done.1, bf16[512,1024]{1,0:T(8,128)(2,1)S(1)} %convolution_convert_fusion, f32[1024]{0:T(1024)S(1)} %copy-done.8, f32[64,8]{1,0:T(8,128)S(1)} %copy.21, ...), kind=kLoop, calls=%fused_computation.48 | loop fusion | flops 5242880 | bytes 5253124 | tf_op jit(solution)/shard_map/mul | solution.py:24
  187.5 0.0 copy-done.9
  187.5 16.5 %fusion.17 = bf16[512,1024]{1,0:T(8,128)(2,1)S(1)} fusion(bf16[1024,2048]{1,0:T(8,128)(2,1)} %bitcast.54, bf16[1024,2048]{1,0:T(8,128)(2,1)} %bitcast.53, f32[2048]{0:T(1024)S(1)} %copy-done.9, f32[512,1024]{1,0:T(8,128)} %broadcast_multiply_fusion), kind=kOutput, calls=%fused_computation.36 | convolution fusion | flops 4365221888 | bytes 11542528 | tf_op jit(solution)/shard_map/dot_general | solution.py:278
  204.0 0.0 copy-start.5
  204.0 1.0 copy-done.5
  205.0 0.8 constant_dynamic-slice_fusion
  205.8 0.9 collective-permute-start.2
  206.7 12.7 %collective-permute-done.2 = bf16[256,1024]{1,0:T(8,128)(2,1)S(1)} collective-permute-done((bf16[256,1024]{1,0:T(8,128)(2,1)}, bf16[256,1024]{1,0:T(8,128)(2,1)S(1)}, u32[]{:S(2)}, u32[]{:S(2)}) %collective-permute-start.2) | collective-permute-done | bytes 524320 | tf_op jit(solution)/shard_map/ppermute | solution.py:20
  219.4 1.3 multiply_reduce_fusion.3
  220.7 0.0 copy-done.4
  220.7 0.0 copy-done.7
  220.7 1.5 multiply_reduce_fusion.2
  222.2 1.4 fusion.22
  223.6 2.1 collective-permute-start.3
  225.7 0.0 collective-permute-start.4
  227.0 14.2 %collective-permute-done.3 = bf16[32,8,1024]{2,1,0:T(8,128)(2,1)S(1)} collective-permute-done((bf16[32,8,1024]{2,1,0:T(8,128)(2,1)S(1)}, bf16[32,8,1024]{2,1,0:T(8,128)(2,1)S(1)}, u32[]{:S(2)}, u32[]{:S(2)}) %collective-permute-start.3) | collective-permute-done | bytes 524320 | tf_op jit(solution)/shard_map/ppermute | solution.py:20
  241.2 3.3 %collective-permute-done.4 = bf16[32,8,1024]{2,1,0:T(8,128)(2,1)S(1)} collective-permute-done((bf16[32,8,1024]{2,1,0:T(8,128)(2,1)S(1)}, bf16[32,8,1024]{2,1,0:T(8,128)(2,1)S(1)}, u32[]{:S(2)}, u32[]{:S(2)}) %collective-permute-start.4) | collective-permute-done | bytes 524320 | tf_op jit(solution)/shard_map/ppermute | solution.py:20
  244.5 1.4 fusion.27
  (8 shorter events, 0.0 us)
Async XLA Ops:
  3.5 1.0 copy-start
  4.6 0.9 copy-start.1
  5.5 0.9 copy-start.2
  6.5 0.8 copy-start.3
  142.0 3.0 %collective-permute-start = (bf16[2,512,512]{2,1,0:T(8,128)(2,1)}, bf16[2,512,512]{2,1,0:T(8,128)(2,1)S(1)}, u32[]{:S(2)}, u32[]{:S(2)}) collective-permute-start(bf16[2,512,512]{2,1,0:T(8,128)(2,1)} %get-tuple-element.15.refs_0_), channel_id=1, source_target_pairs={{0,1},{1,0},{2,3},{3,2},{4,5},{5,4},{6,7},{7,6},{8,9},{9,8},{10,11... | collective-permute-start | bytes 3145736 | tf_op jit(solution)/shard_map/ppermute | solution.py:263
  145.0 1.0 copy-start.6
  146.0 34.8 %copy-start.8 = (f32[1024]{0:T(1024)S(1)}, f32[1024]{0:T(1024)}, u32[]{:S(2)}) copy-start(f32[1024]{0:T(1024)} %param.17) | copy-start | bytes 12292
  154.8 25.5 %collective-permute-start.1 = (bf16[512,1024]{1,0:T(8,128)(2,1)S(1)}, bf16[512,1024]{1,0:T(8,128)(2,1)S(1)}, u32[]{:S(2)}, u32[]{:S(2)}) collective-permute-start(bf16[512,1024]{1,0:T(8,128)(2,1)S(1)} %convolution_convert_fusion), channel_id=1, source_target_pairs={{0,16},{16,0},{1,17},{17,1},{2,18},{18,2},{3,19},{19,3},{4,20},{20... | collective-permute-start | bytes 3145736 | tf_op jit(solution)/shard_map/ppermute | solution.py:20
  180.8 6.7 %copy-start.9 = (f32[2048]{0:T(1024)S(1)}, f32[2048]{0:T(1024)}, u32[]{:S(2)}) copy-start(f32[2048]{0:T(1024)} %param.19) | copy-start | bytes 24580
  187.5 33.2 %copy-start.4 = (f32[512,1024]{1,0:T(8,128)S(1)}, f32[512,1024]{1,0:T(8,128)}, u32[]{:S(2)}) copy-start(f32[512,1024]{1,0:T(8,128)} %broadcast_multiply_fusion) | copy-start | bytes 6291460
  187.5 33.2 %copy-start.7 = (f32[1024]{0:T(1024)S(1)}, f32[1024]{0:T(1024)}, u32[]{:S(2)}) copy-start(f32[1024]{0:T(1024)} %param.18) | copy-start | bytes 12292
  204.0 1.0 copy-start.5
  205.8 13.6 %collective-permute-start.2 = (bf16[256,1024]{1,0:T(8,128)(2,1)}, bf16[256,1024]{1,0:T(8,128)(2,1)S(1)}, u32[]{:S(2)}, u32[]{:S(2)}) collective-permute-start(bf16[256,1024]{1,0:T(8,128)(2,1)} %constant_dynamic-slice_fusion), channel_id=1, source_target_pairs={{0,16},{16,0},{1,17},{17,1},{2,18},{18,2},{3,19},{19,3},{4,20},{20... | collective-permute-start | bytes 1572872 | tf_op jit(solution)/shard_map/ppermute | solution.py:20
  223.6 17.5 %collective-permute-start.3 = (bf16[32,8,1024]{2,1,0:T(8,128)(2,1)S(1)}, bf16[32,8,1024]{2,1,0:T(8,128)(2,1)S(1)}, u32[]{:S(2)}, u32[]{:S(2)}) collective-permute-start(bf16[32,8,1024]{2,1,0:T(8,128)(2,1)S(1)} %fusion.22), channel_id=1, source_target_pairs={{0,2},{1,3},{2,4},{3,5},{4,6},{5,7},{6,8},{7,9},{8,10},{9,11},{10,... | collective-permute-start | bytes 1572872 | tf_op jit(solution)/shard_map/ppermute | solution.py:20
  225.7 18.8 %collective-permute-start.4 = (bf16[32,8,1024]{2,1,0:T(8,128)(2,1)S(1)}, bf16[32,8,1024]{2,1,0:T(8,128)(2,1)S(1)}, u32[]{:S(2)}, u32[]{:S(2)}) collective-permute-start(bf16[32,8,1024]{2,1,0:T(8,128)(2,1)S(1)} %fusion.22), channel_id=1, source_target_pairs={{0,1},{1,2},{2,3},{3,4},{4,5},{5,6},{6,7},{7,8},{8,9},{9,10},{10,1... | collective-permute-start | bytes 1572872 | tf_op jit(solution)/shard_map/ppermute | solution.py:20
where the time goes:
time: 247 us; the launch traced here: 246 us
  Pallas kernels  132 us (53%)
  waiting for transfers between devices  56 us (23%)
  other arithmetic  18.3 us (7%)
  matrix products  18.3 us (7%)
  local copies, waits for them, and re-layouts  11 us (4%)
  between operations  5.71 us (2%)
  starting transfers between devices  4.43 us (2%)
    pallas_call x1, Pallas kernels, gather_all(): pl.pallas_call(functools.partial(gather_kernel, n_row, n_col, reach, n_we...  115 us
    ppermute x4, waiting for transfers between devices, shifted(): return lax.ppermute(value, axis, pairs)  54.7 us
    dot_general x1, matrix products, on_device(): lax.dot_general(activated, down_full, contract, preferred_element_type=jn...  16.5 us
    pallas_call x1, Pallas kernels, project(): pl.pallas_call(functools.partial(project_kernel, heads), grid=(tokens //...  10.1 us
    reduce_sum x5, other arithmetic, to_sphere(): jnp.mean(vector * vector, axis=-1, keepdims=True) + 1e-06  8.07 us
    pallas_call x1, Pallas kernels, attend(): pl.pallas_call(functools.partial(attend_kernel, heads), grid=(tokens // b...  7.01 us
    unnamed x20, local copies, waits for them, and re-layouts  5.73 us
  transfers between devices with their start and end apart: 5, of which 5 were waited for; matrix products, arithmetic and copies ran while one was open for 0% of the time, Pallas kernels for 0%

commit v1 on v0

v1 whole, which is shorter than its diff:
```python
import functools
import math

import jax
import jax.numpy as jnp
from jax import lax
from jax.experimental import pallas as pl
from jax.experimental.pallas import tpu as pltpu
from jax.sharding import PartitionSpec as P

HD = 64
WIN = 16
MESH = pl.DeviceIdType.MESH
VMEM = pl.BlockSpec(memory_space=pltpu.VMEM)


def shifted(value, axis, steps):
    count = lax.axis_size(axis)
    pairs = [(source, (source + steps) % count) for source in range(count)]
    return lax.ppermute(value, axis, pairs)


def to_sphere(vector):
    return vector * lax.rsqrt(jnp.mean(vector * vector, axis=-1, keepdims=True) + 1e-06)


class Ring:
    def __init__(self, n_row, n_col, send_sem, recv_sem):
        self.n_row, self.n_col, self.nz = n_row, n_col, n_col // 4
        self.send_sem, self.recv_sem = send_sem, recv_sem
        self.row, self.col = lax.axis_index("row"), lax.axis_index("col")
        self.z, self.y, self.core = self.col // 4, (self.col // 2) % 2, self.col % 2
        self.z_next = (self.row, self.at(self.z + 1, self.y, self.core))
        self.z_prev = (self.row, self.at(self.z - 1, self.y, self.core))
        self.y_peer = (self.row, self.at(self.z, 1 - self.y, self.core))
        self.core_peer = (self.row, self.at(self.z, self.y, 1 - self.core))
        self.started, self.core_copies, self.z_copy, self.y_copy = [], [], {}, {}

    def at(self, z, y, core):
        return (lax.rem(z + 2 * self.nz, self.nz) * 2 + y) * 2 + core

    def other_row(self, r):
        return (lax.rem(self.row + r, self.n_row), self.col)

    def greet(self, more):
        peers = [self.z_next, self.z_prev, self.y_peer, self.core_peer] + more
        peers += [self.other_row(r) for r in range(1, self.n_row)]
        barrier = pltpu.get_barrier_semaphore()
        for peer in peers:
            pl.semaphore_signal(barrier, inc=1, device_id=peer, device_id_type=MESH)
        pl.semaphore_wait(barrier, len(peers))

    def send(self, src, dst, peer):
        index = len(self.started)
        copy = pltpu.make_async_remote_copy(
            src_ref=src,
            dst_ref=dst,
            send_sem=self.send_sem.at[index],
            recv_sem=self.recv_sem.at[index],
            device_id=peer,
            device_id_type=MESH,
        )
        copy.start()
        self.started.append(copy)
        return copy

    def begin(self, w_in, w_out):
        for w in range(len(w_in)):
            slot = w_out[w].at[self.col]
            self.z_copy[w, 0] = self.send(w_in[w], slot, self.z_next)
            self.y_copy[w, 0] = self.send(w_in[w], slot, self.y_peer)
            self.core_copies.append(self.send(w_in[w], slot, self.core_peer))
        for w in range(len(w_in)):
            w_out[w][self.col] = w_in[w][...]

    def advance(self, t, w_out):
        for w in range(len(w_out)):
            if t > 0:
                self.z_copy[w, t - 1].wait_recv()
                block = w_out[w].at[self.at(self.z - t, self.y, self.core)]
                if t < self.nz - 1:
                    self.z_copy[w, t] = self.send(block, block, self.z_next)
                self.y_copy[w, t] = self.send(block, block, self.y_peer)
                self.core_copies.append(self.send(block, block, self.core_peer))
        for w in range(len(w_out)):
            self.y_copy[w, t].wait_recv()
            other = w_out[w].at[self.at(self.z - t, 1 - self.y, self.core)]
            self.core_copies.append(self.send(other, other, self.core_peer))

    def finish(self):
        for copy in self.core_copies:
            copy.wait_recv()
        for copy in self.started:
            copy.wait_send()


def gather_kernel(n_row, n_col, reach, n_weights, *refs):
    tok_in = refs[0]
    w_in = refs[1 : 1 + n_weights]
    tok_out = refs[1 + n_weights]
    w_out = refs[2 + n_weights : 2 + 2 * n_weights]
    ring = Ring(n_row, n_col, *refs[2 + 2 * n_weights :])
    row, col = ring.row, ring.col
    ring.greet(
        [(row, lax.rem(col + k, n_col)) for k in range(1, reach + 1)]
        + [(row, lax.rem(col - k + n_col, n_col)) for k in range(1, reach + 1)]
    )
    near = {}
    far = []
    for k in range(1, reach + 1):
        near[k] = ring.send(tok_in, tok_out.at[row, k], (row, lax.rem(col - k + n_col, n_col)))
    for r in range(1, n_row):
        far.append(ring.send(tok_in, tok_out.at[row, 0], ring.other_row(r)))
    ring.begin(w_in, w_out)
    tok_out[row, 0] = tok_in[...]
    for t in range(ring.nz):
        if t == 1:
            for k in range(1, reach + 1):
                near[k].wait_recv()
                piece = tok_out.at[row, k]
                for r in range(1, n_row):
                    far.append(ring.send(piece, piece, ring.other_row(r)))
        ring.advance(t, w_out)
    for copy in far:
        copy.wait_recv()
    ring.finish()


def ring_copies(n_col, n_weights):
    nz = n_col // 4
    return n_weights * (nz - 1 + nz + 2 * nz)


def gather_all(tokens, weights, n_row, n_col, reach):
    n_weights = len(weights)
    copies = reach * n_row + (n_row - 1) + ring_copies(n_col, n_weights)
    return pl.pallas_call(
        functools.partial(gather_kernel, n_row, n_col, reach, n_weights),
        out_shape=[jax.ShapeDtypeStruct((n_row, reach + 1) + tokens.shape, tokens.dtype)]
        + [jax.ShapeDtypeStruct((n_col,) + w.shape, w.dtype) for w in weights],
        in_specs=[VMEM] * (1 + n_weights),
        out_specs=[VMEM] * (1 + n_weights),
        scratch_shapes=[pltpu.SemaphoreType.DMA((copies,)), pltpu.SemaphoreType.DMA((copies,))],
        compiler_params=pltpu.CompilerParams(
            collective_id=0, has_side_effects=True, vmem_limit_bytes=48 * 1024 * 1024
        ),
        name="gather_all",
    )(tokens, *weights)


def attention_kernel(n_row, n_col, per_window, heads, band, n_weights, *refs):
    x_ref, qkv_ref, out_w_ref, gain_ref = refs[:4]
    w_in = refs[4 : 4 + n_weights]
    terms = refs[4 + n_weights]
    w_out = refs[5 + n_weights : 5 + 2 * n_weights]
    q_all, kv_all, sem_a, sem_b, kv_send, kv_recv, row_send, row_recv = refs[5 + 2 * n_weights :]
    ring = Ring(n_row, n_col, sem_a, sem_b)
    row, col = ring.row, ring.col
    bands = x_ref.shape[0] // band
    width = heads * HD
    contract = (((1,), (1,)), ((), ()))
    seat = lax.rem(col, per_window)

    def mate(k):
        return (row, col - seat + lax.rem(seat + k, per_window))

    ring.greet([mate(k) for k in range(1, per_window)])
    ring.begin(w_in, w_out)

    def band_rows(b):
        return pl.ds(pl.multiple_of(b * band, band), band)

    def kv_copy(b, k):
        return pltpu.make_async_remote_copy(
            src_ref=kv_all.at[0, :, band_rows(b)],
            dst_ref=kv_all.at[k, :, band_rows(b)],
            send_sem=kv_send.at[b, k],
            recv_sem=kv_recv.at[b, k],
            device_id=mate(k),
            device_id_type=MESH,
        )

    def row_copy(b, r):
        return pltpu.make_async_remote_copy(
            src_ref=terms.at[0, band_rows(b)],
            dst_ref=terms.at[r, band_rows(b)],
            send_sem=row_send.at[b, r],
            recv_sem=row_recv.at[b, r],
            device_id=ring.other_row(r),
            device_id_type=MESH,
        )

    def project(b, carry):
        here = band_rows(b)
        projected = jnp.dot(x_ref[here, :], qkv_ref[...], preferred_element_type=jnp.float32)
        for part in range(2):
            for head in range(heads):
                lo = head * HD
                piece = projected[:, part * width + lo : part * width + lo + HD]
                scaled = (to_sphere(piece) * gain_ref[:, lo : lo + HD]).astype(jnp.bfloat16)
                if part == 0:
                    q_all[here, lo : lo + HD] = scaled
                else:
                    kv_all[0, 0, here, lo : lo + HD] = scaled
        kv_all[0, 1, here, :] = projected[:, 2 * width :].astype(jnp.bfloat16)
        for k in range(1, per_window):
            kv_copy(b, k).start()
        return carry

    lax.fori_loop(0, bands, project, 0)
    for t in range(ring.nz // 2):
        ring.advance(t, w_out)

    def attend(b, carry):
        here = band_rows(b)
        for k in range(1, per_window):
            kv_copy(b, k).wait_recv()
        outs = []
        for head in range(heads):
            cut = slice(head * HD, head * HD + HD)
            query = q_all[here, cut]
            keys = jnp.concatenate([kv_all[k, 0, here, cut] for k in range(per_window)], axis=0)
            values = jnp.concatenate([kv_all[k, 1, here, cut] for k in range(per_window)], axis=0)
            scores = lax.dot_general(query, keys, contract, preferred_element_type=jnp.float32)
            expo = jnp.exp(scores * (1.0 / math.sqrt(HD)))
            weights = (expo / jnp.sum(expo, axis=-1, keepdims=True)).astype(jnp.bfloat16)
            outs.append(
                jnp.dot(weights, values, preferred_element_type=jnp.float32).astype(jnp.bfloat16)
            )
        attended = jnp.concatenate(outs, axis=1)
        terms[0, here, :] = lax.dot_general(
            attended, out_w_ref[...], contract, preferred_element_type=jnp.float32
        ).astype(jnp.bfloat16)
        for r in range(1, n_row):
            row_copy(b, r).start()
        return carry

    lax.fori_loop(0, bands, attend, 0)
    for t in range(ring.nz // 2, ring.nz):
        ring.advance(t, w_out)
    ring.finish()

    def drain(b, carry):
        for k in range(1, per_window):
            kv_copy(b, k).wait_send()
        for r in range(1, n_row):
            row_copy(b, r).wait()
        return carry

    lax.fori_loop(0, bands, drain, 0)


def attention(x, qkv, out_w, gain, weights, n_row, n_col, per_window, band):
    tokens, depth = x.shape
    width = qkv.shape[1] // 3
    heads = width // HD
    bands = tokens // band
    n_weights = len(weights)
    copies = ring_copies(n_col, n_weights)
    dma = pltpu.SemaphoreType.DMA
    return pl.pallas_call(
        functools.partial(attention_kernel, n_row, n_col, per_window, heads, band, n_weights),
        out_shape=[jax.ShapeDtypeStruct((n_row, tokens, depth), jnp.bfloat16)]
        + [jax.ShapeDtypeStruct((n_col,) + w.shape, w.dtype) for w in weights],
        in_specs=[VMEM] * (4 + n_weights),
        out_specs=[VMEM] * (1 + n_weights),
        scratch_shapes=[
            pltpu.VMEM((tokens, width), jnp.bfloat16),
            pltpu.VMEM((per_window, 2, tokens, width), jnp.bfloat16),
            dma((copies,)),
            dma((copies,)),
            dma((bands, per_window)),
            dma((bands, per_window)),
            dma((bands, n_row)),
            dma((bands, n_row)),
        ],
        compiler_params=pltpu.CompilerParams(
            collective_id=1, has_side_effects=True, vmem_limit_bytes=56 * 1024 * 1024
        ),
        name="attention",
    )(x, qkv, out_w, gain.reshape(1, width), *weights)


def on_device(
    tokens,
    shifts,
    qkv_weight,
    out_weight,
    up_weight,
    down_weight,
    qk_gain,
    attn_rate,
    mlp_rate,
    hidden_gain,
):
    n_row = lax.axis_size("row")
    n_col = lax.axis_size("col")
    row = lax.axis_index("row")
    local_rows, cols, width = tokens.shape
    local_width = qkv_weight.shape[2]
    hidden = up_weight.shape[1]
    per_window = WIN // cols
    reach = (WIN + cols - 2) // cols
    strip_rows = local_rows * n_row
    count = strip_rows * cols
    shift_row, shift_col = shifts[0], shifts[1]

    gathered = gather_all(
        tokens.reshape(local_rows * cols, width),
        [qkv_weight.reshape(-1, 3 * local_width), out_weight.T],
        n_row,
        n_col,
        reach,
    )
    pieces = gathered[0].reshape(n_row, reach + 1, local_rows, cols, width)
    qkv_full = gathered[1].reshape(width, 3 * local_width)
    out_full = gathered[2].reshape(width, local_width)

    wide = pieces.transpose(0, 2, 1, 3, 4).reshape(strip_rows, (reach + 1) * cols, width)
    strip = lax.dynamic_slice_in_dim(wide, shift_col, cols, axis=1)
    strip = jnp.roll(strip, -shift_row, axis=0).reshape(count, width)
    flat = to_sphere(strip.astype(jnp.float32))
    second = attention(
        flat.astype(jnp.bfloat16),
        qkv_full,
        out_full,
        qk_gain,
        [up_weight, down_weight.T],
        n_row,
        n_col,
        per_window,
        WIN * cols,
    )
    terms = second[0]
    up_full = second[1].reshape(width, hidden)
    down_full = second[2].reshape(width, hidden)
    attn_all = terms[0].astype(jnp.float32)
    for r in range(1, n_row):
        attn_all = attn_all + terms[r].astype(jnp.float32)
    mixed = to_sphere(flat + attn_rate * (to_sphere(attn_all) - flat))
    raised = jnp.dot(mixed.astype(jnp.bfloat16), up_full, preferred_element_type=jnp.float32)
    activated = jax.nn.gelu(raised * hidden_gain, approximate=False).astype(jnp.bfloat16)
    mlp_own = lax.dot_general(
        activated, down_full, (((1,), (1,)), ((), ())), preferred_element_type=jnp.float32
    ).astype(jnp.bfloat16)

    def part(value, owner):
        lifted = value.reshape(strip_rows, cols, width)
        twice = jnp.concatenate([lifted, lifted], axis=0)
        first = jnp.mod(owner * local_rows - shift_row, strip_rows)
        return lax.dynamic_slice_in_dim(twice, first, local_rows, 0)

    mlp_local = part(mlp_own, row).astype(jnp.float32)
    for r in range(1, n_row):
        there = part(mlp_own, lax.rem(row + r, n_row))
        mlp_local = mlp_local + shifted(there, "row", r).astype(jnp.float32)
    mixed_local = part(mixed, row)
    result = to_sphere(mixed_local + mlp_rate * (to_sphere(mlp_local) - mixed_local))
    result = result.astype(jnp.bfloat16)
    spread = [shifted(result, "col", k) for k in range(reach, 0, -1)] + [result]
    spread = jnp.concatenate(spread, axis=1)
    return lax.dynamic_slice_in_dim(spread, reach * cols - shift_col, cols, axis=1)


def solution(mesh):
    return jax.shard_map(
        on_device,
        mesh=mesh,
        in_specs=(
            P("row", "col", None),
            P(),
            P("col", None, "row"),
            P("row", "col"),
            P("col", "row"),
            P("row", "col"),
            P("row"),
            P(),
            P(),
            P("row"),
        ),
        out_specs=P("row", "col", None),
        check_vma=False,
    )
```

time: 247 us -> 199 us (0.81)
  waiting for transfers between devices: 56 us -> 31.8 us
  Pallas kernels: 132 us -> 122 us
  local copies, waits for them, and re-layouts: 11 us -> 6.05 us
  other arithmetic: 18.3 us -> 14.3 us
    pallas_call x1, Pallas kernels: 115 us -> 53.5 us  [gather_all(): pl.pallas_call(functools.partial(gather_kernel, n_row, n_col, reach, n_we...]
    pallas_call x2 -> x1, Pallas kernels: 17.2 us -> 68.2 us  [attention(): pl.pallas_call(functools.partial(attention_kernel, n_row, n_col, per_wind...]
    ppermute x4 -> x3, waiting for transfers between devices: 54.7 us -> 31.8 us  [shifted(): return lax.ppermute(value, axis, pairs)]
    unnamed x20 -> x16, local copies, waits for them, and re-layouts: 5.73 us -> 2.88 us
    reshape x2 -> x0, other arithmetic: 2.85 us -> none  [the longest x1 1.45 us: on_device(): jnp.roll(normed.astype(jnp.bfloat16), -shift_row, axis=0)]
    dot_general x2 -> x1, matrix products: 18.3 us -> 16.4 us  [on_device(): lax.dot_general(activated, down_full, (((1,), (1,)), ((), ())), preferred...]
  transfers between devices with their start and end apart: 5 -> 3, of which waited for: 5 -> 3; matrix products, arithmetic and copies ran while one was open for 0% -> 0% of each run, Pallas kernels for 0% -> 0%
where the time goes in v1:
time: 199 us; the launch traced here: 198 us
  Pallas kernels  122 us (61%)
  waiting for transfers between devices  31.8 us (16%)
  matrix products  16.4 us (8%)
  other arithmetic  14.3 us (7%)
  local copies, waits for them, and re-layouts  6.05 us (3%)
  between operations  5.53 us (3%)
  starting transfers between devices  2.73 us (1%)
    pallas_call x1, Pallas kernels, attention(): pl.pallas_call(functools.partial(attention_kernel, n_row, n_col, per_wind...  68.2 us
    pallas_call x1, Pallas kernels, gather_all(): pl.pallas_call(functools.partial(gather_kernel, n_row, n_col, reach, n_we...  53.5 us
    ppermute x3, waiting for transfers between devices, shifted(): return lax.ppermute(value, axis, pairs)  31.8 us
    dot_general x1, matrix products, on_device(): lax.dot_general(activated, down_full, (((1,), (1,)), ((), ())), preferred...  16.4 us
    reduce_sum x5, other arithmetic, to_sphere(): jnp.mean(vector * vector, axis=-1, keepdims=True) + 1e-06  8.36 us
  transfers between devices with their start and end apart: 3, of which 3 were waited for; matrix products, arithmetic and copies ran while one was open for 0% of the time, Pallas kernels for 0%

profile of v1, /device:TPU:0, one launch (start us, length us, event | category | flops | bytes accessed | tf_op | source)
XLA Modules:
  0.0 198.4 jit_solution(12695761549120802775)
XLA Ops:
  0.0 1.3 fusion.60
  4.3 0.9 copy.15
  5.3 0.0 copy-start.1
  5.3 1.0 copy-done.1
  6.3 0.0 copy-start.2
  6.3 0.8 copy-done.2
  7.1 53.5 %gather_all.1 = (bf16[2,3,256,1024]{3,2,1,0:T(8,128)(2,1)S(1)}, bf16[16,64,1536]{2,1,0:T(8,128)(2,1)}, bf16[16,64,512]{2,1,0:T(8,128)(2,1)S(1)}) custom-call(bf16[256,1024]{1,0:T(8,128)(2,1)S(1)} %bitcast.41, bf16[64,1536]{1,0:T(8,128)(2,1)S(1)} %bitcast.40, bf16[64,512]{1,0:T(8,128)(2,1)S(1)} %bitcast.42), custom_call_target="tpu_custom_call" | custom-call | tf_op jit(solution)/shard_map/gather_all/pallas_call | solution.py:137
  60.7 0.0 copy-start
  60.7 1.0 copy-done
  61.7 0.3 copy.14
  62.6 0.5 constant_dynamic-slice_fusion
  63.0 0.6 fusion.13
  63.7 0.1 rsqrt.48
  63.7 1.2 fusion.15.refs_0_
  65.0 0.0 copy-start.5
  65.0 68.2 %attention.1 = (bf16[2,512,1024]{2,1,0:T(8,128)(2,1)}, bf16[16,64,2048]{2,1,0:T(8,128)(2,1)}, bf16[16,64,2048]{2,1,0:T(8,128)(2,1)}) custom-call(bf16[512,1024]{1,0:T(8,128)(2,1)} %fusion.15.refs_0_, bf16[1024,1536]{1,0:T(8,128)(2,1)} %bitcast.44, bf16[1024,512]{1,0:T(8,128)(2,1)} %bitcast.39, f32[1,512]{1,0:T(1,128)} %bitcast.47, bf16[64,2048]{1,0:T(8,128)(2,1)} %refs_4_.1, ...), custom_call_target="tpu_custom_call" | custom-call | tf_op jit(solution)/shard_map/attention/pallas_call | solution.py:261
  133.1 0.0 copy-start.3
  133.1 2.1 %multiply_reduce_fusion.1 = f32[512]{0:T(512)S(1)} fusion(bf16[2,512,1024]{2,1,0:T(8,128)(2,1)} %get-tuple-element.14), kind=kLoop, calls=%fused_computation.38 | loop fusion | flops 2620928 | bytes 2099200 | tf_op jit(solution)/shard_map/reduce_sum | solution.py:24
  135.2 0.1 rsqrt.50
  135.3 0.0 copy-done.5
  135.4 0.0 copy-start.7
  135.4 2.4 %multiply_reduce_fusion = f32[64,8]{1,0:T(8,128)S(1)} fusion(f32[64,8]{1,0:T(8,128)S(1)} %rsqrt.50, bf16[2,512,1024]{2,1,0:T(8,128)(2,1)} %get-tuple-element.14, f32[1024]{0:T(1024)S(1)} %copy-done.5, f32[64,8]{1,0:T(8,128)S(1)} %add_rsqrt_fusion.1, bf16[64,8,1024]{2,1,0:T(8,128)(2,1)S(1)} %get-tuple-element.20), kind=kLoop, calls=%fused_computation.37 | loop fusion | flops 5766656 | bytes 3155968 | tf_op jit(solution)/shard_map/reduce_sum | solution.py:24
  137.8 0.0 copy-done.3
  137.8 2.1 %broadcast_multiply_fusion = f32[64,8,1024]{2,1,0:T(8,128)} fusion(f32[64,8]{1,0:T(8,128)S(1)} %add_rsqrt_fusion, f32[64,8]{1,0:T(8,128)S(1)} %rsqrt.50, bf16[2,512,1024]{2,1,0:T(8,128)(2,1)S(1)} %copy-done.3, f32[1024]{0:T(1024)S(1)} %copy-done.5, f32[64,8]{1,0:T(8,128)S(1)} %add_rsqrt_fusion.1, bf16[64,8,1024]{2,1,0:T(8,128)(2,1)S(1)} %get-tuple-element.20), kind=kLoop, calls=%fused_computation.55 | loop fusion | flops 5242880 | bytes 5253120 | tf_op jit(solution)/shard_map/mul | solution.py:24
  139.9 0.0 copy-done.7
  139.9 0.0 copy-start.6
  139.9 16.4 %fusion.18 = bf16[64,8,1024]{2,1,0:T(8,128)(2,1)S(1)} fusion(bf16[1024,2048]{1,0:T(8,128)(2,1)} %bitcast.49, bf16[1024,2048]{1,0:T(8,128)(2,1)} %bitcast.48, f32[2048]{0:T(1024)S(1)} %copy-done.7, f32[64,8,1024]{2,1,0:T(8,128)} %broadcast_multiply_fusion), kind=kOutput, calls=%fused_computation.45 | convolution fusion | flops 4365221888 | bytes 11542528 | tf_op jit(solution)/shard_map/dot_general | solution.py:343
  156.3 0.0 copy-start.4
  156.3 1.0 fusion.27
  157.4 1.6 collective-permute-start
  159.6 12.4 %collective-permute-done = bf16[32,8,1024]{2,1,0:T(8,128)(2,1)} collective-permute-done((bf16[32,8,1024]{2,1,0:T(8,128)(2,1)}, bf16[32,8,1024]{2,1,0:T(8,128)(2,1)}, u32[]{:S(2)}, u32[]{:S(2)}) %collective-permute-start) | collective-permute-done | bytes 524320 | tf_op jit(solution)/shard_map/ppermute | solution.py:20
  171.9 1.4 multiply_reduce_fusion.3
  173.4 0.0 copy-done.6
  173.4 0.0 copy-done.4
  173.4 1.8 multiply_reduce_fusion.2
  175.2 0.1 multiply_convert_fusion
  175.3 1.2 collective-permute-start.1
  176.5 0.0 collective-permute-start.2
  177.6 15.2 %collective-permute-done.1 = bf16[32,8,1024]{2,1,0:T(8,128)(2,1)S(1)} collective-permute-done((bf16[32,8,1024]{2,1,0:T(8,128)(2,1)S(1)}, bf16[32,8,1024]{2,1,0:T(8,128)(2,1)S(1)}, u32[]{:S(2)}, u32[]{:S(2)}) %collective-permute-start.1) | collective-permute-done | bytes 524320 | tf_op jit(solution)/shard_map/ppermute | solution.py:20
  192.9 4.2 %collective-permute-done.2 = bf16[32,8,1024]{2,1,0:T(8,128)(2,1)S(1)} collective-permute-done((bf16[32,8,1024]{2,1,0:T(8,128)(2,1)S(1)}, bf16[32,8,1024]{2,1,0:T(8,128)(2,1)S(1)}, u32[]{:S(2)}, u32[]{:S(2)}) %collective-permute-start.2) | collective-permute-done | bytes 524320 | tf_op jit(solution)/shard_map/ppermute | solution.py:20
  197.1 1.4 fusion.26
  (5 shorter events, 0.1 us)
Async XLA Ops:
  5.3 1.0 copy-start.1
  6.3 0.8 copy-start.2
  60.7 1.0 copy-start
  65.0 70.4 %copy-start.5 = (f32[1024]{0:T(1024)S(1)}, f32[1024]{0:T(1024)}, u32[]{:S(2)}) copy-start(f32[1024]{0:T(1024)} %param.17) | copy-start | bytes 12292
  133.1 4.7 %copy-start.3 = (bf16[2,512,1024]{2,1,0:T(8,128)(2,1)S(1)}, bf16[2,512,1024]{2,1,0:T(8,128)(2,1)}, u32[]{:S(2)}) copy-start(bf16[2,512,1024]{2,1,0:T(8,128)(2,1)} %get-tuple-element.14) | copy-start | bytes 6291460
  135.4 4.6 %copy-start.7 = (f32[2048]{0:T(1024)S(1)}, f32[2048]{0:T(1024)}, u32[]{:S(2)}) copy-start(f32[2048]{0:T(1024)} %param.19) | copy-start | bytes 24580
  139.9 33.5 %copy-start.6 = (f32[1024]{0:T(1024)S(1)}, f32[1024]{0:T(1024)}, u32[]{:S(2)}) copy-start(f32[1024]{0:T(1024)} %param.18) | copy-start | bytes 12292
  156.3 17.1 %copy-start.4 = (f32[64,8,1024]{2,1,0:T(8,128)S(1)}, f32[64,8,1024]{2,1,0:T(8,128)}, u32[]{:S(2)}) copy-start(f32[64,8,1024]{2,1,0:T(8,128)} %broadcast_multiply_fusion) | copy-start | bytes 6291460
  157.4 14.6 %collective-permute-start = (bf16[32,8,1024]{2,1,0:T(8,128)(2,1)}, bf16[32,8,1024]{2,1,0:T(8,128)(2,1)}, u32[]{:S(2)}, u32[]{:S(2)}) collective-permute-start(bf16[32,8,1024]{2,1,0:T(8,128)(2,1)} %fusion.27), channel_id=1, source_target_pairs={{0,16},{16,0},{1,17},{17,1},{2,18},{18,2},{3,19},{19,3},{4,20},{20... | collective-permute-start | bytes 1572872 | tf_op jit(solution)/shard_map/ppermute | solution.py:20
  175.3 17.5 %collective-permute-start.1 = (bf16[32,8,1024]{2,1,0:T(8,128)(2,1)S(1)}, bf16[32,8,1024]{2,1,0:T(8,128)(2,1)S(1)}, u32[]{:S(2)}, u32[]{:S(2)}) collective-permute-start(bf16[32,8,1024]{2,1,0:T(8,128)(2,1)S(1)} %multiply_convert_fusion), channel_id=1, source_target_pairs={{0,2},{1,3},{2,4},{3,5},{4,6},{5,7},{6,8},{7,9},{8,10},{9,11},{10,... | collective-permute-start | bytes 1572872 | tf_op jit(solution)/shard_map/ppermute | solution.py:20
  176.5 20.6 %collective-permute-start.2 = (bf16[32,8,1024]{2,1,0:T(8,128)(2,1)S(1)}, bf16[32,8,1024]{2,1,0:T(8,128)(2,1)S(1)}, u32[]{:S(2)}, u32[]{:S(2)}) collective-permute-start(bf16[32,8,1024]{2,1,0:T(8,128)(2,1)S(1)} %multiply_convert_fusion), channel_id=1, source_target_pairs={{0,1},{1,2},{2,3},{3,4},{4,5},{5,6},{6,7},{7,8},{8,9},{9,10},{10,1... | collective-permute-start | bytes 1572872 | tf_op jit(solution)/shard_map/ppermute | solution.py:20

commit v2 on v1

--- a/solution.py
+++ b/solution.py
@@ -82,10 +82,12 @@
                     self.z_copy[w, t] = self.send(block, block, self.z_next)
                 self.y_copy[w, t] = self.send(block, block, self.y_peer)
                 self.core_copies.append(self.send(block, block, self.core_peer))
-        for w in range(len(w_out)):
-            self.y_copy[w, t].wait_recv()
-            other = w_out[w].at[self.at(self.z - t, 1 - self.y, self.core)]
-            self.core_copies.append(self.send(other, other, self.core_peer))
+        last = t == self.nz - 1
+        for late in ([t - 1] if t > 0 else []) + ([t] if last else []):
+            for w in range(len(w_out)):
+                self.y_copy[w, late].wait_recv()
+                other = w_out[w].at[self.at(self.z - late, 1 - self.y, self.core)]
+                self.core_copies.append(self.send(other, other, self.core_peer))
 
     def finish(self):
         for copy in self.core_copies:
@@ -338,11 +340,13 @@
     for r in range(1, n_row):
         attn_all = attn_all + terms[r].astype(jnp.float32)
     mixed = to_sphere(flat + attn_rate * (to_sphere(attn_all) - flat))
-    raised = jnp.dot(mixed.astype(jnp.bfloat16), up_full, preferred_element_type=jnp.float32)
-    activated = jax.nn.gelu(raised * hidden_gain, approximate=False).astype(jnp.bfloat16)
-    mlp_own = lax.dot_general(
-        activated, down_full, (((1,), (1,)), ((), ())), preferred_element_type=jnp.float32
-    ).astype(jnp.bfloat16)
+
+    def feed_forward(rows):
+        raised = jnp.dot(rows, up_full, preferred_element_type=jnp.float32)
+        activated = jax.nn.gelu(raised * hidden_gain, approximate=False).astype(jnp.bfloat16)
+        return lax.dot_general(
+            activated, down_full, (((1,), (1,)), ((), ())), preferred_element_type=jnp.float32
+        ).astype(jnp.bfloat16)
 
     def part(value, owner):
         lifted = value.reshape(strip_rows, cols, width)
@@ -350,10 +354,17 @@
         first = jnp.mod(owner * local_rows - shift_row, strip_rows)
         return lax.dynamic_slice_in_dim(twice, first, local_rows, 0)
 
-    mlp_local = part(mlp_own, row).astype(jnp.float32)
+    mixed_bf = mixed.astype(jnp.bfloat16)
+    own = part(mixed_bf, row).reshape(local_rows * cols, width)
+    moved = []
     for r in range(1, n_row):
-        there = part(mlp_own, lax.rem(row + r, n_row))
-        mlp_local = mlp_local + shifted(there, "row", r).astype(jnp.float32)
+        there = feed_forward(part(mixed_bf, lax.rem(row + r, n_row)).reshape(own.shape))
+        own, there = lax.optimization_barrier((own, there))
+        moved.append(shifted(there, "row", r))
+    mlp_local = feed_forward(own).astype(jnp.float32)
+    for arrived in moved:
+        mlp_local = mlp_local + arrived.astype(jnp.float32)
+    mlp_local = mlp_local.reshape(local_rows, cols, width)
     mixed_local = part(mixed, row)
     result = to_sphere(mixed_local + mlp_rate * (to_sphere(mlp_local) - mixed_local))
     result = result.astype(jnp.bfloat16)

time: 199 us -> 190 us (0.955)
  Pallas kernels: 122 us -> 110 us
  matrix products: 16.4 us -> 20.9 us
  other arithmetic: 14.3 us -> 11.4 us
    pallas_call x1, Pallas kernels: 68.2 us -> 60.1 us  [attention(): pl.pallas_call(functools.partial(attention_kernel, n_row, n_col, per_wind...]
    dot_general x1 -> x2, matrix products: 16.4 us -> 20.9 us  [feed_forward(): lax.dot_general(activated, down_full, (((1,), (1,)), ((), ())), preferred...]
    reduce_sum x5 -> x4, other arithmetic: 8.36 us -> 4.08 us  [to_sphere(): jnp.mean(vector * vector, axis=-1, keepdims=True) + 1e-06]
    pallas_call x1, Pallas kernels: 53.5 us -> 49.6 us  [gather_all(): pl.pallas_call(functools.partial(gather_kernel, n_row, n_col, reach, n_we...]
    convert_element_type x0 -> x1, other arithmetic: none -> 2.51 us  [on_device(): mixed_bf = mixed.astype(jnp.bfloat16)]
    mul x1 -> x0, other arithmetic: 2.11 us -> none  [to_sphere(): vector * lax.rsqrt(jnp.mean(vector * vector, axis=-1, keepdims=True) + 1e...]
    reshape x0 -> x1, other arithmetic: none -> 2.07 us  [on_device(): own = part(mixed_bf, row).reshape(local_rows * cols, width)]
where the time goes in v2:
time: 190 us; the launch traced here: 189 us
  Pallas kernels  110 us (58%)
  waiting for transfers between devices  33.1 us (17%)
  matrix products  20.9 us (11%)
  other arithmetic  11.4 us (6%)
  between operations  6.29 us (3%)
  local copies, waits for them, and re-layouts  6.26 us (3%)
    pallas_call x1, Pallas kernels, attention(): pl.pallas_call(functools.partial(attention_kernel, n_row, n_col, per_wind...  60.1 us
    pallas_call x1, Pallas kernels, gather_all(): pl.pallas_call(functools.partial(gather_kernel, n_row, n_col, reach, n_we...  49.6 us
    ppermute x3, waiting for transfers between devices, shifted(): return lax.ppermute(value, axis, pairs)  33.1 us
    dot_general x2, matrix products, feed_forward(): lax.dot_general(activated, down_full, (((1,), (1,)), ((), ())), preferred...  20.9 us
    reduce_sum x4, other arithmetic, to_sphere(): jnp.mean(vector * vector, axis=-1, keepdims=True) + 1e-06  4.08 us
  transfers between devices with their start and end apart: 3, of which 3 were waited for; matrix products, arithmetic and copies ran while one was open for 0% of the time, Pallas kernels for 0%

profile of v2, /device:TPU:0, one launch (start us, length us, event | category | flops | bytes accessed | tf_op | source)
XLA Modules:
  0.0 189.4 jit_solution(17597819534605262658)
XLA Ops:
  0.0 1.4 fusion.173
  5.4 0.9 copy.15
  6.4 0.0 copy-start.1
  6.4 1.0 copy-done.1
  7.4 0.0 copy-start.2
  7.4 0.8 copy-done.2
  8.3 49.6 %gather_all.1 = (bf16[2,3,256,1024]{3,2,1,0:T(8,128)(2,1)S(1)}, bf16[16,64,1536]{2,1,0:T(8,128)(2,1)}, bf16[16,64,512]{2,1,0:T(8,128)(2,1)S(1)}) custom-call(bf16[256,1024]{1,0:T(8,128)(2,1)S(1)} %bitcast.54, bf16[64,1536]{1,0:T(8,128)(2,1)S(1)} %bitcast.53, bf16[64,512]{1,0:T(8,128)(2,1)S(1)} %bitcast.55), custom_call_target="tpu_custom_call" | custom-call | tf_op jit(solution)/shard_map/gather_all/pallas_call | solution.py:139
  57.8 0.0 copy-start
  57.9 1.0 copy-done
  58.8 0.3 copy.14
  59.9 0.5 constant_dynamic-slice_fusion
  60.3 0.6 fusion.3
  61.0 0.1 rsqrt.51
  61.1 1.2 fusion.5.refs_0_
  62.3 60.1 %attention.1 = (bf16[2,512,1024]{2,1,0:T(8,128)(2,1)}, bf16[16,64,2048]{2,1,0:T(8,128)(2,1)}, bf16[16,64,2048]{2,1,0:T(8,128)(2,1)}) custom-call(bf16[512,1024]{1,0:T(8,128)(2,1)} %fusion.5.refs_0_, bf16[1024,1536]{1,0:T(8,128)(2,1)} %bitcast.57, bf16[1024,512]{1,0:T(8,128)(2,1)} %bitcast.52, f32[1,512]{1,0:T(1,128)} %bitcast.60, bf16[64,2048]{1,0:T(8,128)(2,1)} %refs_4_.1, ...), custom_call_target="tpu_custom_call" | custom-call | tf_op jit(solution)/shard_map/attention/pallas_call | solution.py:263
  122.4 0.0 copy-start.3
  122.4 0.0 copy-start.5
  122.4 2.1 %multiply_reduce_fusion.1 = f32[512]{0:T(512)S(1)} fusion(bf16[2,512,1024]{2,1,0:T(8,128)(2,1)} %get-tuple-element.16), kind=kLoop, calls=%fused_computation.55 | loop fusion | flops 2620928 | bytes 2099200 | tf_op jit(solution)/shard_map/reduce_sum | solution.py:24
  124.5 0.1 rsqrt.53
  124.6 0.0 copy-done.3
  124.6 0.0 copy-done.5
  124.6 0.9 multiply_reduce_fusion
  125.5 0.0 copy-start.7
  125.6 2.5 %fusion.171 = (bf16[64,8,1024]{2,1,0:T(8,128)(2,1)}, f32[64,8,1024]{2,1,0:T(8,128)}) fusion(f32[64,8]{1,0:T(8,128)S(1)} %add_rsqrt_fusion, f32[64,8]{1,0:T(8,128)S(1)} %rsqrt.53, bf16[2,512,1024]{2,1,0:T(8,128)(2,1)S(1)} %copy-done.3, f32[1024]{0:T(1024)S(1)} %copy-done.5, f32[64,8]{1,0:T(8,128)S(1)} %add_rsqrt_fusion.1, ...), kind=kLoop, calls=%fused_computation.214 | loop fusion | flops 5767168 | bytes 6301696 | tf_op jit(solution)/shard_map/convert_element_type | solution.py:357
  128.1 2.1 %fusion.105 = bf16[256,1024]{1,0:T(8,128)(2,1)} fusion(s32[]{:T(128)S(6)} %select_n.42, bf16[64,8,1024]{2,1,0:T(8,128)(2,1)} %get-tuple-element.23), kind=kLoop, calls=%fused_computation.145 | loop fusion | flops 262144 | bytes 1572868 | tf_op jit(solution)/shard_map/reshape | solution.py:358
  130.1 0.0 copy-done.7
  130.1 10.3 %convolution_convert_fusion.1 = bf16[256,1024]{1,0:T(8,128)(2,1)S(1)} fusion(bf16[1024,2048]{1,0:T(8,128)(2,1)} %bitcast.63, bf16[1024,2048]{1,0:T(8,128)(2,1)} %bitcast.61, f32[2048]{0:T(1024)S(1)} %copy-done.7, s32[]{:T(128)S(6)} %select_n.44, bf16[64,8,1024]{2,1,0:T(8,128)(2,1)} %get-tuple-element.23), kind=kOutput, calls=%fused_computation.66 | convolution fusion | flops 2182610944 | bytes 9969668 | tf_op jit(solution)/shard_map/dot_general | solution.py:347
  140.5 0.0 copy-start.4
  140.5 0.0 copy-start.6
  140.5 1.5 collective-permute-start
  142.0 12.9 %collective-permute-done = bf16[256,1024]{1,0:T(8,128)(2,1)} collective-permute-done((bf16[256,1024]{1,0:T(8,128)(2,1)S(1)}, bf16[256,1024]{1,0:T(8,128)(2,1)}, u32[]{:S(2)}, u32[]{:S(2)}) %collective-permute-start) | collective-permute-done | bytes 524320 | tf_op jit(solution)/shard_map/ppermute | solution.py:20
  154.9 10.6 %multiply_reduce_fusion.3 = (f32[256]{0:T(256)S(1)}, f32[256,1024]{1,0:T(8,128)S(1)}) fusion(bf16[256,1024]{1,0:T(8,128)(2,1)} %collective-permute-done, bf16[1024,2048]{1,0:T(8,128)(2,1)} %bitcast.64, bf16[256,1024]{1,0:T(8,128)(2,1)} %fusion.105, bf16[1024,2048]{1,0:T(8,128)(2,1)} %bitcast.62, f32[2048]{0:T(1024)S(1)} %copy-done.7), kind=kOutput, calls=%fused_computation.75 | convolution fusion | flops 2183659264 | bytes 10494976 | tf_op jit(solution)/shard_map/dot_general | solution.py:347
  165.5 0.1 rsqrt.56
  165.6 0.0 copy-done.4
  165.6 0.0 copy-done.6
  165.6 0.5 multiply_reduce_fusion.2
  166.1 0.1 multiply_convert_fusion
  166.2 0.1 collective-permute-start.1
  166.3 0.1 collective-permute-start.2
  167.7 16.0 %collective-permute-done.1 = bf16[32,8,1024]{2,1,0:T(8,128)(2,1)S(1)} collective-permute-done((bf16[32,8,1024]{2,1,0:T(8,128)(2,1)S(1)}, bf16[32,8,1024]{2,1,0:T(8,128)(2,1)S(1)}, u32[]{:S(2)}, u32[]{:S(2)}) %collective-permute-start.1) | collective-permute-done | bytes 524320 | tf_op jit(solution)/shard_map/ppermute | solution.py:20
  183.8 4.2 %collective-permute-done.2 = bf16[32,8,1024]{2,1,0:T(8,128)(2,1)S(1)} collective-permute-done((bf16[32,8,1024]{2,1,0:T(8,128)(2,1)S(1)}, bf16[32,8,1024]{2,1,0:T(8,128)(2,1)S(1)}, u32[]{:S(2)}, u32[]{:S(2)}) %collective-permute-start.2) | collective-permute-done | bytes 524320 | tf_op jit(solution)/shard_map/ppermute | solution.py:20
  188.0 1.4 fusion.99
  (5 shorter events, 0.1 us)
Async XLA Ops:
  6.4 1.0 copy-start.1
  7.4 0.8 copy-start.2
  57.8 1.0 copy-start
  122.4 2.2 %copy-start.3 = (bf16[2,512,1024]{2,1,0:T(8,128)(2,1)S(1)}, bf16[2,512,1024]{2,1,0:T(8,128)(2,1)}, u32[]{:S(2)}) copy-start(bf16[2,512,1024]{2,1,0:T(8,128)(2,1)} %get-tuple-element.16) | copy-start | bytes 6291460
  122.4 2.2 %copy-start.5 = (f32[1024]{0:T(1024)S(1)}, f32[1024]{0:T(1024)}, u32[]{:S(2)}) copy-start(f32[1024]{0:T(1024)} %param.17) | copy-start | bytes 12292
  125.5 4.6 %copy-start.7 = (f32[2048]{0:T(1024)S(1)}, f32[2048]{0:T(1024)}, u32[]{:S(2)}) copy-start(f32[2048]{0:T(1024)} %param.19) | copy-start | bytes 24580
  140.5 25.1 %copy-start.4 = (f32[64,8,1024]{2,1,0:T(8,128)S(1)}, f32[64,8,1024]{2,1,0:T(8,128)}, u32[]{:S(2)}) copy-start(f32[64,8,1024]{2,1,0:T(8,128)} %get-tuple-element.24) | copy-start | bytes 6291460
  140.5 25.1 %copy-start.6 = (f32[1024]{0:T(1024)S(1)}, f32[1024]{0:T(1024)}, u32[]{:S(2)}) copy-start(f32[1024]{0:T(1024)} %param.18) | copy-start | bytes 12292
  140.5 14.4 %collective-permute-start = (bf16[256,1024]{1,0:T(8,128)(2,1)S(1)}, bf16[256,1024]{1,0:T(8,128)(2,1)}, u32[]{:S(2)}, u32[]{:S(2)}) collective-permute-start(bf16[256,1024]{1,0:T(8,128)(2,1)S(1)} %convolution_convert_fusion.1), channel_id=1, source_target_pairs={{0,16},{16,0},{1,17},{17,1},{2,18},{18,2},{3,19},{19,3},{4,20},{20... | collective-permute-start | bytes 1572872 | tf_op jit(solution)/shard_map/ppermute | solution.py:20
  166.2 17.5 %collective-permute-start.1 = (bf16[32,8,1024]{2,1,0:T(8,128)(2,1)S(1)}, bf16[32,8,1024]{2,1,0:T(8,128)(2,1)S(1)}, u32[]{:S(2)}, u32[]{:S(2)}) collective-permute-start(bf16[32,8,1024]{2,1,0:T(8,128)(2,1)S(1)} %multiply_convert_fusion), channel_id=1, source_target_pairs={{0,2},{1,3},{2,4},{3,5},{4,6},{5,7},{6,8},{7,9},{8,10},{9,11},{10,... | collective-permute-start | bytes 1572872 | tf_op jit(solution)/shard_map/ppermute | solution.py:20
  166.3 21.7 %collective-permute-start.2 = (bf16[32,8,1024]{2,1,0:T(8,128)(2,1)S(1)}, bf16[32,8,1024]{2,1,0:T(8,128)(2,1)S(1)}, u32[]{:S(2)}, u32[]{:S(2)}) collective-permute-start(bf16[32,8,1024]{2,1,0:T(8,128)(2,1)S(1)} %multiply_convert_fusion), channel_id=1, source_target_pairs={{0,1},{1,2},{2,3},{3,4},{4,5},{5,6},{6,7},{7,8},{8,9},{9,10},{10,1... | collective-permute-start | bytes 1572872 | tf_op jit(solution)/shard_map/ppermute | solution.py:20
